TPU v7x, 256 devices: a whole 4x4x8 slice. The times are simulated.
256 devices in a mesh: seq: 16 (over z, core), head: 16 (over x, y).
Axes of the slice: x: 4, y: 4, z: 8, core: 2. Of those that a mesh axis runs over, the one named last changes fastest.
Arguments:
- grad_output: bfloat16 [16384, 4096], P('seq', 'head'), may hold values from -6 to 6
- out_weight: bfloat16 [4096, 8192], P('seq', 'head'), may hold values from -0.0625 to 0.0625
- ssd_out: bfloat16 [16384, 8192], P('seq', 'head'), may hold values from -520 to 520
- gate: bfloat16 [16384, 8192], P('seq', 'head'), may hold values from -5 to 5
- norm_weight: float32 [8192], P('head'), may hold values from 0.5 to 1.5
- time_step: float32 [128, 16384], P('head', 'seq'), may hold values from 0.01 to 0.1
- log_decay: float32 [128, 16384], P('head', 'seq'), may hold values from -0.7 to 0
- state_in: bfloat16 [16384, 8, 128], P('seq'), may hold values from -1.796875 to 1.796875
- state_out: bfloat16 [16384, 8, 128], P('seq'), may hold values from -1.796875 to 1.796875
- skip: float32 [128], P('head'), may hold values from 0.5 to 1.5
Outputs:
- grad_x: bfloat16 [16384, 8192], P('seq', 'head')
- grad_gate: bfloat16 [16384, 8192], P('seq', 'head')
- grad_out_weight: float32 [4096, 8192], P('seq', 'head')
All inputs are finite; a program needn't handle non-finite values.
Results may differ from a plain program's by a relative error of at most 0.014.
Values may be sent and summed in bfloat16 or wider, within the bound.
A program may use at most 128 MiB of HBM per device.

v0:
```python
import math
import jax
import jax.numpy as jnp
from jax import lax
from jax.sharding import Mesh
from jax.sharding import PartitionSpec as P

HEADS = 128
GROUPS = 8
BLOCK_LEN = 256
HEAD = ("head_0", "head_1")
SEQ = ("seq_0", "seq_1")
epsilon = 1e-05


def over_axes(x, axes):
    for axis in axes:
        x = lax.psum(x, axis)
    return x


def nothing_yet(x, identity):
    return jax.tree.map(
        lambda part, zero: jnp.zeros_like(part) + jnp.asarray(zero, part.dtype), x, identity
    )


def carried_in(x, axes, combine, identity):
    before = start = nothing_yet(x, identity)
    running = x
    for axis in reversed(axes):
        size, here = (lax.axis_size(axis), lax.axis_index(axis))
        pieces = jax.tree.map(lambda part: lax.all_gather(part, axis), running)
        inside, running = (start, start)
        for k in reversed(range(size)):
            passed = k > here
            running = combine(running, jax.tree.map(lambda part: part[k], pieces))
            inside = jax.tree.map(lambda new, old: jnp.where(passed, new, old), running, inside)
        before = combine(inside, before)
    return before


def on_device(
    grad_output,
    out_weight,
    ssd_out,
    gate,
    norm_weight,
    time_step,
    log_decay,
    state_in,
    state_out,
    skip,
):
    tok_rows = ssd_out.shape[0]
    local_width = ssd_out.shape[1]
    total_width = local_width * lax.axis_size(HEAD)
    full_grad = lax.all_gather(grad_output, HEAD, axis=1, tiled=True)
    values = ssd_out.astype(jnp.float32)
    gate_values = gate.astype(jnp.float32)
    sigmoid_gate = jax.nn.sigmoid(gate_values)
    silu_gate = gate_values * sigmoid_gate
    gated_values = values * silu_gate
    local_squares = jnp.sum(gated_values * gated_values, axis=1)
    columns = full_grad
    normed_grad = jnp.dot(
        columns,
        lax.all_gather(out_weight, SEQ, axis=0, tiled=True),
        preferred_element_type=jnp.float32,
    )
    squares = over_axes(local_squares, HEAD)
    weighted = over_axes(jnp.sum(norm_weight * normed_grad * gated_values, axis=1), HEAD)
    inverse_rms = lax.rsqrt(squares[:, None] / total_width + epsilon)
    normed = (gated_values * inverse_rms * norm_weight).astype(jnp.bfloat16)
    gated_grad = (
        inverse_rms * norm_weight * normed_grad
        - gated_values * inverse_rms**3 * weighted[:, None] / total_width
    )
    grad_gate = (
        gated_grad * values * sigmoid_gate * (1.0 + gate_values * (1.0 - sigmoid_gate))
    ).astype(jnp.bfloat16)
    grad_ssd = (gated_grad * silu_gate).astype(jnp.bfloat16)
    columns = full_grad
    weight_sum = lax.psum_scatter(
        lax.dot_general(
            columns, normed, (((0,), (0,)), ((), ())), preferred_element_type=jnp.float32
        ).astype(jnp.bfloat16),
        SEQ,
        scatter_dimension=0,
        tiled=True,
    ).astype(jnp.float32)
    grad_out_weight = weight_sum * (1.0 / math.sqrt(tok_rows * lax.axis_size(SEQ)))
    heads_here = time_step.shape[0]
    head_width = local_width // heads_here
    blocks = tok_rows // BLOCK_LEN
    state_width = state_in.shape[2]
    group_count = state_in.shape[1]
    first_head = lax.axis_index(HEAD) * heads_here
    head_ids = first_head + jnp.arange(heads_here, dtype=jnp.int32)
    group_ids = head_ids // (HEADS // GROUPS)
    group_pick = (group_ids[:, None] == jnp.arange(group_count, dtype=jnp.int32)[None, :]).astype(
        jnp.bfloat16
    )
    b_heads = jnp.einsum(
        "tgn,hg->htn", state_in, group_pick, preferred_element_type=jnp.float32
    ).astype(jnp.bfloat16)
    b_heads = b_heads.reshape(heads_here, blocks, BLOCK_LEN, state_width)
    c_heads = jnp.einsum(
        "tgn,hg->htn", state_out, group_pick, preferred_element_type=jnp.float32
    ).astype(jnp.bfloat16)
    c_heads = c_heads.reshape(heads_here, blocks, BLOCK_LEN, state_width)
    grad_heads = grad_ssd.reshape(tok_rows, heads_here, head_width).transpose(1, 0, 2)
    grad_heads = grad_heads.reshape(heads_here, blocks, BLOCK_LEN, head_width)
    cumulative = jnp.cumsum(log_decay.reshape(heads_here, blocks, BLOCK_LEN), axis=2)
    block_total = cumulative[..., -1]
    sequence_indices = jnp.arange(BLOCK_LEN)
    upper_mask = sequence_indices[None, :] >= sequence_indices[:, None]
    scores = jnp.einsum("hktn,hksn->hkts", b_heads, c_heads, preferred_element_type=jnp.float32)
    log_gap = cumulative[..., None, :] - cumulative[..., :, None]
    block_weights = jnp.where(upper_mask, scores * jnp.exp(jnp.minimum(log_gap, 0.0)), 0.0).astype(
        jnp.bfloat16
    )
    within = jnp.einsum(
        "hkts,hksp->hktp", block_weights, grad_heads, preferred_element_type=jnp.float32
    )
    grad_float = grad_heads.astype(jnp.float32)
    scaled = (jnp.exp(cumulative)[..., None] * grad_float).astype(jnp.bfloat16)
    block_state = jnp.einsum("hksp,hksn->hkpn", scaled, c_heads, preferred_element_type=jnp.float32)

    def fold_block(carried, inputs):
        state_now, total_now = inputs
        return (state_now + jnp.exp(total_now)[:, None, None] * carried, carried)

    zero_state = jnp.zeros((heads_here, head_width, state_width), jnp.float32)
    summary, inside = lax.scan(
        fold_block, zero_state, (block_state.transpose(1, 0, 2, 3), block_total.T), reverse=True
    )
    decay_total = jnp.exp(jnp.sum(block_total, axis=1))
    tail_decay = jnp.exp(
        jnp.sum(block_total, axis=1, keepdims=True) - jnp.cumsum(block_total, axis=1)
    )

    def combine_pair(earlier, later):
        return (later[0] * earlier[0], later[1] + later[0][:, None, None] * earlier[1])

    identity = (jnp.ones((heads_here,), jnp.float32), zero_state)
    prefix = carried_in((decay_total, summary), SEQ, combine_pair, identity)
    remote = prefix[1]
    full_states = inside.transpose(1, 0, 2, 3) + tail_decay[..., None, None] * remote[:, None]
    carry_low = full_states.astype(jnp.bfloat16)
    across = jnp.einsum("hkpn,hktn->hktp", carry_low, b_heads, preferred_element_type=jnp.float32)
    across = across * jnp.exp(block_total[..., None] - cumulative)[..., None]
    step_sizes = time_step.reshape(heads_here, blocks, BLOCK_LEN)
    grad_head = step_sizes[..., None] * (within + across) + skip[:, None, None, None] * grad_float
    grad_x = (
        grad_head.reshape(heads_here, tok_rows, head_width)
        .transpose(1, 0, 2)
        .reshape(tok_rows, local_width)
    )
    return (grad_x.astype(jnp.bfloat16), grad_gate, grad_out_weight)


def solution(mesh):
    finer = Mesh(mesh.devices.reshape(8, 2, 4, 4), ("seq_0", "seq_1", "head_0", "head_1"))
    return jax.shard_map(
        on_device,
        mesh=finer,
        in_specs=(
            P(SEQ, HEAD),
            P(SEQ, HEAD),
            P(SEQ, HEAD),
            P(SEQ, HEAD),
            P(HEAD),
            P(HEAD, SEQ),
            P(HEAD, SEQ),
            P(SEQ, None, None),
            P(SEQ, None, None),
            P(HEAD),
        ),
        out_specs=(P(SEQ, HEAD), P(SEQ, HEAD), P(SEQ, HEAD)),
        check_vma=False,
    )
```

profile of v0, /device:TPU:2, one launch (start us, length us, event | category | flops | bytes accessed | tf_op | source)
XLA Modules:
  0.0 294.2 jit_solution(11251501523468864543)
XLA Ops:
  8.7 1.3 dynamic-slice.1
  10.0 1.3 dynamic-slice
  13.3 2.3 reduce-window.6
  16.2 1.5 copy.74
  17.7 2.6 copy.75
  20.4 2.4 all-reduce
  23.1 2.1 convolution_convert_fusion.1
  25.2 29.5 %all-gather.9.cloned.1.call-done = bf16[4096,512]{1,0:T(8,128)(2,1)} async-done(((bf16[256,512]{1,0:T(8,128)(2,1)}), bf16[4096,512]{1,0:T(8,128)(2,1)}) %all-gather.9.cloned.1.call-update) | async-done | bytes 4194320 | tf_op jit(solution)/shard_map/all_gather | solution.py:68
  54.7 82.9 %all-gather.7.cloned.1.call-done = bf16[1024,4096]{1,0:T(8,128)(2,1)} async-done(((bf16[1024,256]{1,0:T(8,128)(2,1)}), bf16[1024,4096]{1,0:T(8,128)(2,1)}) %all-gather.7.cloned.1.call-update) | async-done | bytes 8388624 | tf_op jit(solution)/shard_map/all_gather | solution.py:58
  137.6 11.3 %multiply_reduce_fusion.1 = (f32[1024]{0:T(1024)S(1)}, f32[1024]{0:T(1024)S(1)}, f32[1024,512]{0,1:T(8,128)}) fusion(bf16[1024,512]{0,1:T(8,128)(2,1)S(1)} %copy.74, bf16[1024,512]{0,1:T(8,128)(2,1)} %copy.75, f32[512]{0:T(512)S(1)} %copy-done.7, bf16[1024,4096]{1,0:T(8,128)(2,1)} %all-gather.7.cloned.1.call-done, ...), kind=kOutput, calls=%fused_computation.32 | convolution fusion | flops 4301256704 | bytes 16787456 | tf_op jit(solution)/shard_map/dot_general | solution.py:66
  148.8 8.7 %all-reduce.3 = (f32[1024]{0:T(1024)S(1)}, f32[1024]{0:T(1024)S(1)}) all-reduce(f32[1024]{0:T(1024)S(1)} %get-tuple-element.160, f32[1024]{0:T(1024)S(1)} %get-tuple-element.159), channel_id=1, replica_groups=mesh['seq_0'=8,'seq_1'=2,'head_0'=4,'head_1'=4] {'head_0'}, use_global_device_ids=true, to_apply=%region_6.0 | all-reduce | flops 2048 | bytes 16384 | tf_op jit(solution)/shard_map/psum | solution.py:18
  157.5 10.2 %all-reduce.2 = (f32[1024]{0:T(1024)S(1)}, f32[1024]{0:T(1024)S(1)}) all-reduce(f32[1024]{0:T(1024)S(1)} %get-tuple-element.175, f32[1024]{0:T(1024)S(1)} %get-tuple-element.176), channel_id=1, replica_groups=mesh['seq_0'=8,'seq_1'=2,'head_0'=4,'head_1'=4] {'head_1'}, use_global_device_ids=true, to_apply=%region_7.8 | all-reduce | flops 2048 | bytes 16384 | tf_op jit(solution)/shard_map/psum | solution.py:18
  167.8 4.7 %fusion.9 = (bf16[1024,512]{0,1:T(8,128)(2,1)}, bf16[1024,512]{0,1:T(8,128)(2,1)S(1)}) fusion(bf16[1024,512]{0,1:T(8,128)(2,1)S(1)} %copy.74, bf16[1024,512]{0,1:T(8,128)(2,1)} %copy.75, f32[1024]{0:T(1024)S(1)} %get-tuple-element.173, f32[1024]{0:T(1024)S(1)} %get-tuple-element.182, f32[1024,512]{0,1:T(8,128)} %get-tuple-element.195, f32[512]{0:T(512)S(1)} %copy-done.7, ...), kind=kLoop, calls=%fused_computation.20 | loop fusion | flops 11534336 | bytes 6305792 | tf_op jit(solution)/shard_map/convert_element_type | solution.py:81
  172.5 1.8 fusion.27
  174.3 4.5 %while.17 = (s32[]{:T(128)}, f32[8,64,128]{2,1,0:T(8,128)S(1)}, f32[4,8,64,128]{3,2,1,0:T(8,128)S(1)}, f32[4,8,64,128]{3,2,0,1:T(8,128)}, f32[4,8]{1,0:T(4,128)S(1)}, /*index=5*/s32[]{:T(128)}, s32[]{:T(128)}, s32[]{:T(128)}) while((s32[]{:T(128)}, f32[8,64,128]{2,1,0:T(8,128)S(1)}, f32[4,8,64,128]{3,2,1,0:T(8,128)S(1)}, ...), condition=%wide.region_9.10_spmd.clone, body=%wide.region_8.9_spmd.clone.sunk | while | flops 262148 | bytes 1310944 | solution.py:135
  174.4 1.1 bitcast_add_fusion.4
  175.5 1.1 bitcast_add_fusion.4
  176.6 1.1 bitcast_add_fusion.4
  177.8 1.1 bitcast_add_fusion.4
  178.8 1.0 copy-done.4
  179.8 2.2 all-gather
  183.0 11.0 %fusion.2 = bf16[4096,512]{0,1:T(8,128)(2,1)} fusion(bf16[1024,4096]{1,0:T(8,128)(2,1)} %all-gather.7.cloned.1.call-done, f32[512]{0:T(512)S(1)} %copy-done.7, bf16[1024,512]{0,1:T(8,128)(2,1)} %copy-done.2, f32[1024]{0:T(1024)S(1)} %get-tuple-element.181, bf16[1024,512]{0,1:T(8,128)(2,1)} %copy.75), kind=kOutput, calls=%fused_computation.7 | convolution fusion | flops 4302307328 | bytes 14686208 | tf_op jit(solution)/shard_map/dot_general | solution.py:85
  194.9 17.7 %all-reduce.1 = f32[64]{0:T(128)S(1)} all-reduce(f32[64]{0:T(128)S(1)} %copy-done.10), channel_id=4, replica_groups=mesh['seq_0'=8,'seq_1'=2,'head_0'=4,'head_1'=4] {'seq_0'}, use_global_device_ids=true, to_apply=%add.1 | all-reduce | flops 64 | bytes 512
  212.7 3.7 %convolution_convert_fusion.2 = bf16[8,1024,128]{2,0,1:T(8,128)(2,1)} fusion(bf16[1024,8,128]{2,1,0:T(8,128)(2,1)} %param.19, s32[8]{0:T(128)S(1)} %and_select_fusion), kind=kOutput, calls=%fused_computation.34 | convolution fusion | flops 17825856 | bytes 4194336 | tf_op jit(solution)/shard_map/tgn,hg->htn/dot_general | solution.py:104
  216.3 2.3 copy.86
  218.6 6.3 %fusion.3 = f32[8,4,256,64]{2,3,1,0:T(8,128)} fusion(f32[8,4,256]{2,1,0:T(4,128)S(1)} %copy.72, pred[256,256]{1,0:T(8,128)(4,1)S(1)} %iota_compare_fusion, bf16[8,4,256,128]{3,0,2,1:T(8,128)(2,1)} %bitcast.136, bf16[8,4,256,128]{3,0,2,1:T(8,128)(2,1)} %bitcast.130, bf16[8,8,4,8,256]{4,3,2,1,0:T(8,128)(2,1)} %bitcast.133), kind=kOutput, calls=%fused_computation.8 | convolution fusion | flops 815792128 | bytes 7438336 | tf_op jit(solution)/shard_map/hkts,hksp->hktp/dot_general | solution.py:123
  224.9 2.1 fusion.53
  227.2 3.3 %fusion.30 = bf16[8,4,8,8,256]{4,3,2,1,0:T(8,128)(2,1)S(1)} fusion(f32[8,4,256,64]{2,3,1,0:T(8,128)} %fusion.3, bf16[8,4,256,128]{3,0,2,1:T(8,128)(2,1)S(1)} %bitcast.131, f32[8]{0:T(128)S(1)} %copy-done.8, f32[8,4,256]{2,1,0:T(4,128)S(1)} %copy.83, f32[8,4,256]{2,1,0:T(4,128)S(1)} %copy.67, bf16[8,8,4,8,256]{4,3,2,1,0:T(8,128)(2,1)} %bitcast.134, ...), kind=kOutput, calls=%fused_computation.42 | convolution fusion | flops 138674176 | bytes 7667872 | tf_op jit(solution)/shard_map/hkpn,hktn->hktp/dot_general | solution.py:151
  230.6 1.3 copy.85
  231.9 53.7 %reduce-scatter.2.cloned.1.call-done = bf16[256,512]{0,1:T(8,128)(2,1)} async-done(((bf16[4096,512]{0,1:T(8,128)(2,1)}), bf16[256,512]{0,1:T(8,128)(2,1)}) %reduce-scatter.2.cloned.1.call-update) | async-done | bytes 262160 | tf_op jit(solution)/shard_map/reduce_scatter | solution.py:84
  285.6 1.0 convert_multiply_fusion.7
  286.6 1.0 copy.87
  (63 shorter events, 5.6 us)
Async XLA Ops:
  7.2 15.9 %copy-start = (bf16[1024,8,128]{2,1,0:T(8,128)(2,1)S(1)}, bf16[1024,8,128]{2,1,0:T(8,128)(2,1)}, u32[]{:S(2)}) copy-start(bf16[1024,8,128]{2,1,0:T(8,128)(2,1)} %param.20) | copy-start | bytes 6291460
  7.2 47.5 %all-gather.9.cloned.1.call-start = ((), (), s32[]{:S(2)}) async-start(), calls=%async_computation.2 | async-start | bytes 4456448 | tf_op jit(solution)/shard_map/all_gather | solution.py:68
  7.9 129.7 %all-gather.7.cloned.1.call-start = ((), (), s32[]{:S(2)}) async-start(), calls=%async_computation.1 | async-start | bytes 8912896 | tf_op jit(solution)/shard_map/all_gather | solution.py:58
  8.7 216.3 %all-gather.11.cloned.1.call-start = ((), (), s32[]{:S(2)}) async-start(), calls=%async_computation.3 | async-start | bytes 2359296 | tf_op jit(solution)/shard_map/all_gather | solution.py:33
  17.7 150.1 %copy-start.2 = (bf16[1024,512]{0,1:T(8,128)(2,1)}, bf16[1024,512]{0,1:T(8,128)(2,1)S(1)}, u32[]{:S(2)}) copy-start(bf16[1024,512]{0,1:T(8,128)(2,1)S(1)} %copy.74) | copy-start | bytes 3145732
  23.1 2.1 copy-start.9
  23.1 114.5 %copy-start.7 = (f32[512]{0:T(512)S(1)}, f32[512]{0:T(512)}, u32[]{:S(2)}) copy-start(f32[512]{0:T(512)} %param.16) | copy-start | bytes 6148
  167.8 4.7 %copy-start.5 = (bf16[8,1024,128]{2,0,1:T(8,128)(2,1)S(1)}, bf16[8,1024,128]{2,0,1:T(8,128)(2,1)}, u32[]{:S(2)}) copy-start(bf16[8,1024,128]{2,0,1:T(8,128)(2,1)} %convolution_convert_fusion.1) | copy-start | bytes 6291460
  172.5 1.8 copy-start.3
  178.8 1.0 copy-start.4
  182.8 102.8 %reduce-scatter.2.cloned.1.call-start = ((), (), s32[]{:S(2)}) async-start(), calls=%async_computation.4 | async-start | bytes 4456448 | tf_op jit(solution)/shard_map/reduce_scatter | solution.py:84
  194.0 0.8 copy-start.6
  194.1 0.8 copy-start.10
  224.9 2.1 copy-start.8
  224.9 2.2 copy-start.1
Sparse Core Ops, SparseCore 0:
  9.8 44.8 all-gather.8
  57.1 80.4 all-gather.6
  182.9 38.5 all-gather.10
  223.9 61.6 reduce-scatter.1
where the time goes:
time: 295 us; the launch traced here: 294 us
  waiting for transfers between devices  167 us (57%)
  blocking collectives  41.2 us (14%)
  matrix products  39.5 us (13%)
  other arithmetic  15.8 us (5%)
  between operations  15.3 us (5%)
  local copies, waits for them, and re-layouts  14.4 us (5%)
    all_gather x1, waiting for transfers between devices, on_device(): full_grad = lax.all_gather(grad_output, HEAD, axis=1, tiled=True)  82.9 us
    reduce_scatter x1, waiting for transfers between devices, on_device(): lax.psum_scatter(lax.dot_general(columns, normed, (((0,), (0,)), ((), ())...  53.7 us
    all_gather x1, waiting for transfers between devices, on_device(): lax.all_gather(out_weight, SEQ, axis=0, tiled=True)  29.5 us
    unnamed x2, blocking collectives  20.1 us
    psum x2, blocking collectives, over_axes(): x = lax.psum(x, axis)  18.9 us
    unnamed x32, local copies, waits for them, and re-layouts  13.2 us
    dot_general x1, matrix products, on_device(): jnp.dot(columns, lax.all_gather(out_weight, SEQ, axis=0, tiled=True), pre...  11.3 us
    dot_general x1, matrix products, on_device(): lax.dot_general(columns, normed, (((0,), (0,)), ((), ())), preferred_elem...  11 us
  transfers between devices with their start and end apart: 4, of which 3 were waited for; matrix products, arithmetic and copies ran while one was open for 15% of the time, Pallas kernels for 0%

commit v1 on v0

--- a/solution.py
+++ b/solution.py
@@ -55,7 +55,9 @@
     tok_rows = ssd_out.shape[0]
     local_width = ssd_out.shape[1]
     total_width = local_width * lax.axis_size(HEAD)
-    full_grad = lax.all_gather(grad_output, HEAD, axis=1, tiled=True)
+    full_grad = jnp.concatenate(
+        lax.all_to_all(jnp.stack([grad_output] * lax.axis_size(HEAD)), HEAD, 0, 0), axis=1
+    )
     values = ssd_out.astype(jnp.float32)
     gate_values = gate.astype(jnp.float32)
     sigmoid_gate = jax.nn.sigmoid(gate_values)

time: 295 us -> 330 us (1.12)
  blocking collectives: 41.2 us -> 89 us
  waiting for transfers between devices: 167 us -> 143 us
  starting transfers between devices: 0.34 us -> 7.78 us
  local copies, waits for them, and re-layouts: 14.4 us -> 18.1 us
    all_to_all x0 -> x1, waiting for transfers between devices: none -> 89.6 us  [on_device(): lax.all_to_all(jnp.stack([grad_output] * lax.axis_size(HEAD)), HEAD, 0, 0)]
    all_gather x1 -> x0, waiting for transfers between devices: 82.9 us -> none  [on_device(): full_grad = lax.all_gather(grad_output, HEAD, axis=1, tiled=True)]
    psum x2, blocking collectives: 18.9 us -> 64.4 us  [over_axes(): x = lax.psum(x, axis)]
    all_gather x1, waiting for transfers between devices: 29.5 us -> 0.01 us  [on_device(): lax.all_gather(out_weight, SEQ, axis=0, tiled=True)]
    all_to_all x0 -> x1, starting transfers between devices: none -> 7.48 us  [on_device(): lax.all_to_all(jnp.stack([grad_output] * lax.axis_size(HEAD)), HEAD, 0, 0)]
    another operation x2 -> x3, local copies, waits for them, and re-layouts: 0.02 us -> 4.31 us  [the longest x1 4.29 us: on_device(): jnp.stack([grad_output] * lax.axis_size(HEAD))]
    unnamed x32 -> x39, local copies, waits for them, and re-layouts: 13.2 us -> 13.3 us
  transfers between devices with their start and end apart: 4 -> 4, of which waited for: 3 -> 2; matrix products, arithmetic and copies ran while one was open for 15% -> 12% of each run, Pallas kernels for 0% -> 0%
where the time goes in v1:
time: 330 us; the launch traced here: 329 us
  waiting for transfers between devices  143 us (43%)
  blocking collectives  89 us (27%)
  matrix products  39.5 us (12%)
  local copies, waits for them, and re-layouts  18.1 us (5%)
  other arithmetic  15.8 us (5%)
  between operations  15.3 us (5%)
  starting transfers between devices  7.78 us (2%)
    all_to_all x1, waiting for transfers between devices, on_device(): lax.all_to_all(jnp.stack([grad_output] * lax.axis_size(HEAD)), HEAD, 0, 0)  89.6 us
    psum x2, blocking collectives, over_axes(): x = lax.psum(x, axis)  64.4 us
    reduce_scatter x1, waiting for transfers between devices, on_device(): lax.psum_scatter(lax.dot_general(columns, normed, (((0,), (0,)), ((), ())...  53.1 us
    unnamed x2, blocking collectives  22.5 us
    unnamed x39, local copies, waits for them, and re-layouts  13.3 us
    dot_general x1, matrix products, on_device(): jnp.dot(columns, lax.all_gather(out_weight, SEQ, axis=0, tiled=True), pre...  11.3 us
    dot_general x1, matrix products, on_device(): lax.dot_general(columns, normed, (((0,), (0,)), ((), ())), preferred_elem...  11 us
    all_to_all x1, starting transfers between devices, on_device(): lax.all_to_all(jnp.stack([grad_output] * lax.axis_size(HEAD)), HEAD, 0, 0)  7.48 us
  transfers between devices with their start and end apart: 4, of which 2 were waited for; matrix products, arithmetic and copies ran while one was open for 12% of the time, Pallas kernels for 0%

profile of v1, /device:TPU:2, one launch (start us, length us, event | category | flops | bytes accessed | tf_op | source)
XLA Modules:
  0.0 329.1 jit_solution(11686139407932693106)
XLA Ops:
  7.2 1.4 copy.78
  8.6 4.3 %stack.2 = bf16[16,1024,256]{1,2,0:T(8,128)(2,1)} broadcast(bf16[1024,256]{0,1:T(8,128)(2,1)S(1)} %copy.78), dimensions={1,2} | broadcast | bytes 8912896 | tf_op jit(solution)/shard_map/stack | solution.py:59
  12.9 7.5 %all-to-all-start = ((bf16[16,1024,256]{1,2,0:T(8,128)(2,1)}), bf16[16,1024,256]{1,2,0:T(8,128)(2,1)}, u32[]{:S(2)}, u32[]{:S(2)}) async-start(bf16[16,1024,256]{1,2,0:T(8,128)(2,1)} %stack.2), calls=%async_computation | async-start | bytes 16777216 | tf_op jit(solution)/shard_map/all_to_all | solution.py:59
  21.2 1.5 copy.76
  22.7 2.6 copy.77
  25.3 2.3 reduce-window.6
  30.8 2.4 all-reduce
  33.5 2.1 convolution_convert_fusion.1
  35.6 89.6 %all-to-all-done = bf16[16,1024,256]{1,2,0:T(8,128)(2,1)} async-done(((bf16[16,1024,256]{1,2,0:T(8,128)(2,1)}), bf16[16,1024,256]{1,2,0:T(8,128)(2,1)}, u32[]{:S(2)}, u32[]{:S(2)}) %all-to-all-start) | async-done | bytes 8388640 | tf_op jit(solution)/shard_map/all_to_all | solution.py:59
  125.2 11.3 %multiply_reduce_fusion.1 = (f32[1024]{0:T(1024)S(1)}, f32[1024]{0:T(1024)S(1)}, f32[1024,512]{0,1:T(8,128)}) fusion(bf16[1024,512]{0,1:T(8,128)(2,1)S(1)} %copy.76, bf16[1024,512]{0,1:T(8,128)(2,1)} %copy.77, f32[512]{0:T(512)S(1)} %copy-done.8, bf16[1024,4096]{0,1:T(8,128)(2,1)} %bitcast.6, bf16[4096,512]{1,0:T(8,128)(2,1)} %all-gather.6.cloned.1.call-done), kind=kOutput, calls=%fused_computation.32 | convolution fusion | flops 4301256704 | bytes 16787456 | tf_op jit(solution)/shard_map/dot_general | solution.py:68
  136.5 50.7 %all-reduce.3 = (f32[1024]{0:T(1024)S(1)}, f32[1024]{0:T(1024)S(1)}) all-reduce(f32[1024]{0:T(1024)S(1)} %get-tuple-element.160, f32[1024]{0:T(1024)S(1)} %get-tuple-element.159), channel_id=1, replica_groups=mesh['seq_0'=8,'seq_1'=2,'head_0'=4,'head_1'=4] {'head_0'}, use_global_device_ids=true, to_apply=%region_6.0 | all-reduce | flops 2048 | bytes 16384 | tf_op jit(solution)/shard_map/psum | solution.py:18
  187.2 13.7 %all-reduce.2 = (f32[1024]{0:T(1024)S(1)}, f32[1024]{0:T(1024)S(1)}) all-reduce(f32[1024]{0:T(1024)S(1)} %get-tuple-element.175, f32[1024]{0:T(1024)S(1)} %get-tuple-element.176), channel_id=1, replica_groups=mesh['seq_0'=8,'seq_1'=2,'head_0'=4,'head_1'=4] {'head_1'}, use_global_device_ids=true, to_apply=%region_7.8 | all-reduce | flops 2048 | bytes 16384 | tf_op jit(solution)/shard_map/psum | solution.py:18
  200.9 4.7 %fusion.9 = (bf16[1024,512]{0,1:T(8,128)(2,1)}, bf16[1024,512]{0,1:T(8,128)(2,1)S(1)}) fusion(bf16[1024,512]{0,1:T(8,128)(2,1)S(1)} %copy.76, bf16[1024,512]{0,1:T(8,128)(2,1)} %copy.77, f32[1024]{0:T(1024)S(1)} %get-tuple-element.173, f32[1024]{0:T(1024)S(1)} %get-tuple-element.182, f32[1024,512]{0,1:T(8,128)} %get-tuple-element.195, f32[512]{0:T(512)S(1)} %copy-done.8, ...), kind=kLoop, calls=%fused_computation.20 | loop fusion | flops 11534336 | bytes 6305792 | tf_op jit(solution)/shard_map/convert_element_type | solution.py:83
  205.6 1.8 fusion.27
  207.5 4.5 %while.17 = (s32[]{:T(128)}, f32[8,64,128]{2,1,0:T(8,128)S(1)}, f32[4,8,64,128]{3,2,1,0:T(8,128)S(1)}, f32[4,8,64,128]{3,2,0,1:T(8,128)}, f32[4,8]{1,0:T(4,128)S(1)}, /*index=5*/s32[]{:T(128)}, s32[]{:T(128)}, s32[]{:T(128)}) while((s32[]{:T(128)}, f32[8,64,128]{2,1,0:T(8,128)S(1)}, f32[4,8,64,128]{3,2,1,0:T(8,128)S(1)}, ...), condition=%wide.region_9.10_spmd.clone, body=%wide.region_8.9_spmd.clone.sunk | while | flops 262148 | bytes 1310936 | solution.py:137
  207.6 1.1 bitcast_add_fusion.4
  208.7 1.1 bitcast_add_fusion.4
  209.8 1.1 bitcast_add_fusion.4
  210.9 1.1 bitcast_add_fusion.4
  212.0 1.0 copy-done.4
  213.0 2.2 all-gather
  216.2 11.0 %fusion.2 = bf16[4096,512]{0,1:T(8,128)(2,1)} fusion(bf16[1024,4096]{0,1:T(8,128)(2,1)} %bitcast.6, f32[512]{0:T(512)S(1)} %copy-done.8, bf16[1024,512]{0,1:T(8,128)(2,1)} %copy-done.2, f32[1024]{0:T(1024)S(1)} %get-tuple-element.181, bf16[1024,512]{0,1:T(8,128)(2,1)} %copy.77), kind=kOutput, calls=%fused_computation.7 | convolution fusion | flops 4302307328 | bytes 14686208 | tf_op jit(solution)/shard_map/dot_general | solution.py:87
  228.0 20.0 %all-reduce.1 = f32[64]{0:T(128)S(1)} all-reduce(f32[64]{0:T(128)S(1)} %copy-done.11), channel_id=4, replica_groups=mesh['seq_0'=8,'seq_1'=2,'head_0'=4,'head_1'=4] {'seq_0'}, use_global_device_ids=true, to_apply=%add.1 | all-reduce | flops 64 | bytes 512
  248.1 3.7 %convolution_convert_fusion.2 = bf16[8,1024,128]{2,0,1:T(8,128)(2,1)} fusion(bf16[1024,8,128]{2,1,0:T(8,128)(2,1)} %param.19, s32[8]{0:T(128)S(1)} %and_select_fusion), kind=kOutput, calls=%fused_computation.34 | convolution fusion | flops 17825856 | bytes 4194336 | tf_op jit(solution)/shard_map/tgn,hg->htn/dot_general | solution.py:106
  251.9 2.3 copy.89
  254.2 6.3 %fusion.3 = f32[8,4,256,64]{2,3,1,0:T(8,128)} fusion(f32[8,4,256]{2,1,0:T(4,128)S(1)} %copy.74, pred[256,256]{1,0:T(8,128)(4,1)S(1)} %iota_compare_fusion, bf16[8,4,256,128]{3,0,2,1:T(8,128)(2,1)} %bitcast.139, bf16[8,4,256,128]{3,0,2,1:T(8,128)(2,1)} %bitcast.133, bf16[8,8,4,8,256]{4,3,2,1,0:T(8,128)(2,1)} %bitcast.136), kind=kOutput, calls=%fused_computation.8 | convolution fusion | flops 815792128 | bytes 7438336 | tf_op jit(solution)/shard_map/hkts,hksp->hktp/dot_general | solution.py:125
  260.4 2.1 fusion.53
  262.7 3.3 %fusion.30 = bf16[8,4,8,8,256]{4,3,2,1,0:T(8,128)(2,1)S(1)} fusion(f32[8,4,256,64]{2,3,1,0:T(8,128)} %fusion.3, bf16[8,4,256,128]{3,0,2,1:T(8,128)(2,1)S(1)} %bitcast.134, f32[8]{0:T(128)S(1)} %copy-done.9, f32[8,4,256]{2,1,0:T(4,128)S(1)} %copy.86, f32[8,4,256]{2,1,0:T(4,128)S(1)} %copy.69, bf16[8,8,4,8,256]{4,3,2,1,0:T(8,128)(2,1)} %bitcast.137, ...), kind=kOutput, calls=%fused_computation.42 | convolution fusion | flops 138674176 | bytes 7667872 | tf_op jit(solution)/shard_map/hkpn,hktn->hktp/dot_general | solution.py:153
  266.1 1.3 copy.88
  267.4 53.1 %reduce-scatter.2.cloned.1.call-done = bf16[256,512]{0,1:T(8,128)(2,1)} async-done(((bf16[4096,512]{0,1:T(8,128)(2,1)}), bf16[256,512]{0,1:T(8,128)(2,1)}) %reduce-scatter.2.cloned.1.call-update) | async-done | bytes 262160 | tf_op jit(solution)/shard_map/reduce_scatter | solution.py:86
  320.6 1.0 convert_multiply_fusion.7
  321.5 1.0 copy.90
  (70 shorter events, 5.3 us)
Async XLA Ops:
  7.2 26.3 %copy-start = (bf16[1024,8,128]{2,1,0:T(8,128)(2,1)S(1)}, bf16[1024,8,128]{2,1,0:T(8,128)(2,1)}, u32[]{:S(2)}) copy-start(bf16[1024,8,128]{2,1,0:T(8,128)(2,1)} %param.20) | copy-start | bytes 6291460
  12.9 112.3 %all-to-all-start = ((bf16[16,1024,256]{1,2,0:T(8,128)(2,1)}), bf16[16,1024,256]{1,2,0:T(8,128)(2,1)}, u32[]{:S(2)}, u32[]{:S(2)}) async-start(bf16[16,1024,256]{1,2,0:T(8,128)(2,1)} %stack.2), calls=%async_computation | async-start | bytes 16777216 | tf_op jit(solution)/shard_map/all_to_all | solution.py:59
  20.3 104.8 %all-gather.6.cloned.1.call-start = ((), (), s32[]{:S(2)}) async-start(), calls=%async_computation.2 | async-start | bytes 4456448 | tf_op jit(solution)/shard_map/all_gather | solution.py:70
  21.1 239.3 %all-gather.8.cloned.1.call-start = ((), (), s32[]{:S(2)}) async-start(), calls=%async_computation.3 | async-start | bytes 2359296 | tf_op jit(solution)/shard_map/all_gather | solution.py:33
  21.1 4.2 %copy-start.6 = (f32[8,1024]{1,0:T(8,128)S(1)}, f32[8,1024]{1,0:T(8,128)}, u32[]{:S(2)}) copy-start(f32[8,1024]{1,0:T(8,128)} %param.18) | copy-start | bytes 98308
  21.2 7.1 %copy-start.13 = (u32[256]{0:T(256)S(1)}, u32[256]{0:T(256)}, u32[]{:S(2)}) copy-start(u32[256]{0:T(256)} %constant.117) | copy-start | bytes 3076
  21.2 7.7 %copy-start.12 = (u32[256]{0:T(256)S(1)}, u32[256]{0:T(256)}, u32[]{:S(2)}) copy-start(u32[256]{0:T(256)} %constant.122) | copy-start | bytes 3076
  22.7 178.2 %copy-start.2 = (bf16[1024,512]{0,1:T(8,128)(2,1)}, bf16[1024,512]{0,1:T(8,128)(2,1)S(1)}, u32[]{:S(2)}) copy-start(bf16[1024,512]{0,1:T(8,128)(2,1)S(1)} %copy.76) | copy-start | bytes 3145732
  33.5 2.1 copy-start.10
  33.5 91.7 %copy-start.8 = (f32[512]{0:T(512)S(1)}, f32[512]{0:T(512)}, u32[]{:S(2)}) copy-start(f32[512]{0:T(512)} %param.16) | copy-start | bytes 6148
  200.9 4.7 %copy-start.5 = (bf16[8,1024,128]{2,0,1:T(8,128)(2,1)S(1)}, bf16[8,1024,128]{2,0,1:T(8,128)(2,1)}, u32[]{:S(2)}) copy-start(bf16[8,1024,128]{2,0,1:T(8,128)(2,1)} %convolution_convert_fusion.1) | copy-start | bytes 6291460
  205.6 1.8 copy-start.3
  212.0 1.0 copy-start.4
  216.0 104.6 %reduce-scatter.2.cloned.1.call-start = ((), (), s32[]{:S(2)}) async-start(), calls=%async_computation.4 | async-start | bytes 4456448 | tf_op jit(solution)/shard_map/reduce_scatter | solution.py:86
  227.2 0.8 copy-start.7
  227.2 0.8 copy-start.11
  260.4 2.1 copy-start.9
  260.4 2.2 copy-start.1
Sparse Core Ops, SparseCore 0:
  23.0 44.4 all-gather.5
  216.1 40.0 all-gather.7
  258.7 61.7 reduce-scatter.1
